TPU v7x, 128 devices: a whole 4x4x4 slice. The times are simulated.
128 devices in a mesh: dp: 1, sp: 64 (over z, y, x), tp: 2 (over core).
Axes of the slice: x: 4, y: 4, z: 4, core: 2. Of those that a mesh axis runs over, the one named last changes fastest.
Arguments:
- hidden_in: bfloat16 [8192, 1536], P(('dp', 'sp', 'tp'))
- segment_ids: int32 [8192], P(('dp', 'sp', 'tp'))
- positions: int32 [8192], P(('dp', 'sp', 'tp'))
- attn_gain: bfloat16 [8, 1536], replicated
- w_q: bfloat16 [8, 1536, 1536], P(None, None, 'tp')
- w_k: bfloat16 [8, 1536, 256], P(None, None, 'tp')
- w_v: bfloat16 [8, 1536, 256], P(None, None, 'tp')
- w_o: bfloat16 [8, 1536, 1536], P(None, 'tp')
- mlp_gain: bfloat16 [8, 1536], replicated
- w_gate: bfloat16 [8, 1536, 8960], P(None, None, 'tp')
- w_up: bfloat16 [8, 1536, 8960], P(None, None, 'tp')
- w_down: bfloat16 [8, 8960, 1536], P(None, 'tp')
Outputs:
- output 1: bfloat16 [8192, 1536], P(('dp', 'sp', 'tp'))
- output 2: bfloat16 [8, 8192, 2, 128], P(None, ('dp', 'sp'), 'tp')
- output 3: bfloat16 [8, 8192, 2, 128], P(None, ('dp', 'sp'), 'tp')
All inputs are finite; a program needn't handle non-finite values.
Results may differ from a plain program's by a relative error of at most 0.02.
Values are sent between devices in bfloat16 or wider.
A program may use at most 1.5 GiB of HBM per device.

v0:
```python
import math
import jax
import jax.numpy as jnp
from jax import lax
from jax.sharding import PartitionSpec as P

HEAD_DIM = 128
ROPE_BASE = 1e4
NORM_EPS = 1e-5
SCORE_SCALE = HEAD_DIM ** -0.5


def rms_norm(hidden, gain_vec):
    hidden32 = hidden.astype(jnp.float32)
    inv_rms = lax.rsqrt(jnp.mean(hidden32 * hidden32, axis=-1, keepdims=True) + NORM_EPS)
    return (hidden32 * inv_rms * gain_vec.astype(jnp.float32)).astype(jnp.bfloat16)


def rotary(rot_in, positions):
    half_dim = HEAD_DIM // 2
    inv_freq = ROPE_BASE ** (-jnp.arange(half_dim, dtype=jnp.float32) / half_dim)
    angles = positions.astype(jnp.float32)[..., None] * inv_freq
    cos_val = jnp.cos(angles)[..., None, :]
    sin_val = jnp.sin(angles)[..., None, :]
    first_half = rot_in[..., :half_dim]
    second_half = rot_in[..., half_dim:]
    return jnp.concatenate([first_half * cos_val - second_half * sin_val, second_half * cos_val + first_half * sin_val], axis=-1)


def attention_rows(q_rot, k_keys, v_keys, row_index, row_seg, key_seg):
    n_rows, n_kv, group_size = q_rot.shape[0], q_rot.shape[1], q_rot.shape[2]
    blk_rows = math.gcd(n_rows, 128)
    n_blocks = n_rows // blk_rows
    key_index = jnp.arange(k_keys.shape[0])

    def one_block(block_in):
        q_blk, idx_blk, seg_blk = block_in
        scores = jnp.einsum('qkgd,skd->kgqs', q_blk, k_keys, preferred_element_type=jnp.float32) * SCORE_SCALE
        allowed = (idx_blk[:, None] >= key_index[None, :]) & (seg_blk[:, None] == key_seg[None, :])
        probs = jax.nn.softmax(jnp.where(allowed, scores, -1e30), axis=-1).astype(jnp.bfloat16)
        return jnp.einsum('kgqs,skd->kgqd', probs, v_keys, preferred_element_type=jnp.float32).astype(jnp.bfloat16)

    blocks = (q_rot.reshape(n_blocks, blk_rows, n_kv, group_size, HEAD_DIM),
              row_index.reshape(n_blocks, blk_rows), row_seg.reshape(n_blocks, blk_rows))
    return lax.map(one_block, blocks)


def solution(mesh):
    n_tp = mesh.shape['tp']
    tok_spec = P(('dp', 'sp', 'tp'))
    col_spec = P(None, None, 'tp')
    row_spec = P(None, 'tp', None)
    cache_spec = P(None, ('dp', 'sp'), 'tp', None)

    def device_fn(hidden_in, segment_ids, positions, attn_gain, w_q, w_k, w_v, w_o, mlp_gain, w_gate, w_up, w_down):
        tok_local, model_dim = hidden_in.shape
        n_rows = tok_local * n_tp
        n_kv = w_k.shape[2] // HEAD_DIM
        group_size = w_q.shape[2] // HEAD_DIM // n_kv
        row_seg = lax.all_gather(segment_ids, 'tp', tiled=True)
        row_pos = lax.all_gather(positions, 'tp', tiled=True)
        key_seg = lax.all_gather(row_seg, 'sp', tiled=True)
        row_index = lax.axis_index('sp') * n_rows + jnp.arange(n_rows)
        hidden = hidden_in
        k_list = []
        v_list = []
        for layer_idx in range(w_q.shape[0]):
            normed = lax.all_gather(rms_norm(hidden, attn_gain[layer_idx]), 'tp', axis=0, tiled=True)
            q_lin = jnp.dot(normed, w_q[layer_idx], preferred_element_type=jnp.float32).reshape(n_rows, n_kv * group_size, HEAD_DIM)
            k_lin = jnp.dot(normed, w_k[layer_idx], preferred_element_type=jnp.float32).reshape(n_rows, n_kv, HEAD_DIM)
            v_rows = jnp.dot(normed, w_v[layer_idx], preferred_element_type=jnp.float32).astype(jnp.bfloat16).reshape(n_rows, n_kv, HEAD_DIM)
            q_rot = rotary(q_lin, row_pos).astype(jnp.bfloat16).reshape(n_rows, n_kv, group_size, HEAD_DIM)
            k_rows = rotary(k_lin, row_pos).astype(jnp.bfloat16)
            k_keys = lax.all_gather(k_rows, 'sp', axis=0, tiled=True)
            v_keys = lax.all_gather(v_rows, 'sp', axis=0, tiled=True)
            att_out = attention_rows(q_rot, k_keys, v_keys, row_index, row_seg, key_seg)
            wo_heads = w_o[layer_idx].reshape(n_kv, group_size, HEAD_DIM, model_dim)
            part_sum = jnp.einsum('nkgqd,kgdm->nqm', att_out, wo_heads, preferred_element_type=jnp.float32).astype(jnp.bfloat16).reshape(n_rows, model_dim)
            attn_res = lax.psum_scatter(part_sum, 'tp', scatter_dimension=0, tiled=True)
            hidden_mid = (hidden.astype(jnp.float32) + attn_res.astype(jnp.float32)).astype(jnp.bfloat16)
            normed_mlp = lax.all_gather(rms_norm(hidden_mid, mlp_gain[layer_idx]), 'tp', axis=0, tiled=True)
            gate_lin = jnp.dot(normed_mlp, w_gate[layer_idx], preferred_element_type=jnp.float32)
            up_lin = jnp.dot(normed_mlp, w_up[layer_idx], preferred_element_type=jnp.float32)
            act_vals = (jax.nn.silu(gate_lin) * up_lin).astype(jnp.bfloat16)
            down_part = jnp.dot(act_vals, w_down[layer_idx], preferred_element_type=jnp.float32).astype(jnp.bfloat16)
            mlp_res = lax.psum_scatter(down_part, 'tp', scatter_dimension=0, tiled=True)
            hidden = (hidden_mid.astype(jnp.float32) + mlp_res.astype(jnp.float32)).astype(jnp.bfloat16)
            k_list.append(k_rows)
            v_list.append(v_rows)
        return hidden, jnp.stack(k_list), jnp.stack(v_list)

    return jax.shard_map(device_fn, mesh=mesh,
                         in_specs=(P(('dp', 'sp', 'tp'), None), tok_spec, tok_spec, P(), col_spec, col_spec, col_spec, row_spec, P(), col_spec, col_spec, row_spec),
                         out_specs=(P(('dp', 'sp', 'tp'), None), cache_spec, cache_spec), check_vma=False)
```

profile of v0, /device:TPU:1, one launch (start us, length us, event | category | flops | bytes accessed | tf_op | source)
XLA Modules:
  0.0 1759.6 jit_solution(17697793452049033815)
XLA Ops:
  24.1 12.6 slice_bitcast_fusion
  44.3 150.5 %all-gather.8 = s32[64,1,128]{2,1,0:T(1,128)S(1)} all-gather(s32[1,1,128]{2,1,0:T(1,128)S(1)} %bitcast.740), channel_id=1, replica_groups=mesh['dp'=1,'sp'=64,'tp'=2] {'sp'}, dimensions={0}, use_global_device_ids=true | all-gather | bytes 33280 | tf_op jit(solution)/shard_map/all_gather | solution.py:62
  200.3 13.4 fusion.552
  236.3 14.3 fusion.153
  251.5 31.4 %reduce-scatter.17.cloned.1.call-done = bf16[64,1536]{1,0:T(8,128)(2,1)} async-done(((bf16[128,1536]{1,0:T(8,128)(2,1)}), bf16[64,1536]{1,0:T(8,128)(2,1)}) %reduce-scatter.17.cloned.1.call-update) | async-done | bytes 196624 | tf_op jit(solution)/shard_map/reduce_scatter | solution.py:79
  296.7 12.7 fusion.161
  309.4 11.9 reduce-scatter.19.cloned.1.call-done
  336.5 58.5 %all-gather.28.cloned.1.call-done = bf16[8192,1,128]{0,2,1:T(8,128)(2,1)} async-done(((bf16[128,1,128]{0,2,1:T(8,128)(2,1)}), bf16[8192,1,128]{0,2,1:T(8,128)(2,1)}) %all-gather.28.cloned.1.call-update) | async-done | bytes 2097168 | tf_op jit(solution)/shard_map/all_gather | solution.py:74
  395.0 12.3 fusion.9
  418.2 43.5 %all-gather.44.cloned.1.call-done = bf16[8192,128]{1,0:T(8,128)(2,1)} async-done(((bf16[128,128]{1,0:T(8,128)(2,1)}), bf16[8192,128]{1,0:T(8,128)(2,1)}) %all-gather.44.cloned.1.call-update) | async-done | bytes 2097168 | tf_op jit(solution)/shard_map/all_gather | solution.py:75
  461.8 14.3 fusion.154
  501.0 12.9 fusion.164
  513.9 11.9 reduce-scatter.23.cloned.1.call-done
  541.0 58.5 %all-gather.30.cloned.1.call-done = bf16[8192,1,128]{0,2,1:T(8,128)(2,1)} async-done(((bf16[128,1,128]{0,2,1:T(8,128)(2,1)}), bf16[8192,1,128]{0,2,1:T(8,128)(2,1)}) %all-gather.30.cloned.1.call-update) | async-done | bytes 2097168 | tf_op jit(solution)/shard_map/all_gather | solution.py:74
  599.5 12.3 fusion.10
  622.8 43.5 %all-gather.46.cloned.1.call-done = bf16[8192,128]{1,0:T(8,128)(2,1)} async-done(((bf16[128,128]{1,0:T(8,128)(2,1)}), bf16[8192,128]{1,0:T(8,128)(2,1)}) %all-gather.46.cloned.1.call-update) | async-done | bytes 2097168 | tf_op jit(solution)/shard_map/all_gather | solution.py:75
  666.3 14.3 fusion.155
  705.3 12.9 fusion.167
  718.2 11.9 reduce-scatter.27.cloned.1.call-done
  745.4 58.4 %all-gather.32.cloned.1.call-done = bf16[8192,1,128]{0,2,1:T(8,128)(2,1)} async-done(((bf16[128,1,128]{0,2,1:T(8,128)(2,1)}), bf16[8192,1,128]{0,2,1:T(8,128)(2,1)}) %all-gather.32.cloned.1.call-update) | async-done | bytes 2097168 | tf_op jit(solution)/shard_map/all_gather | solution.py:74
  803.8 12.3 fusion.11
  827.1 43.5 %all-gather.48.cloned.1.call-done = bf16[8192,128]{1,0:T(8,128)(2,1)} async-done(((bf16[128,128]{1,0:T(8,128)(2,1)}), bf16[8192,128]{1,0:T(8,128)(2,1)}) %all-gather.48.cloned.1.call-update) | async-done | bytes 2097168 | tf_op jit(solution)/shard_map/all_gather | solution.py:75
  870.6 14.3 fusion.156
  909.9 12.9 fusion.170
  922.8 11.9 reduce-scatter.31.cloned.1.call-done
  949.9 58.5 %all-gather.34.cloned.1.call-done = bf16[8192,1,128]{0,2,1:T(8,128)(2,1)} async-done(((bf16[128,1,128]{0,2,1:T(8,128)(2,1)}), bf16[8192,1,128]{0,2,1:T(8,128)(2,1)}) %all-gather.34.cloned.1.call-update) | async-done | bytes 2097168 | tf_op jit(solution)/shard_map/all_gather | solution.py:74
  1008.4 12.3 fusion.12
  1031.6 43.6 %all-gather.50.cloned.1.call-done = bf16[8192,128]{1,0:T(8,128)(2,1)} async-done(((bf16[128,128]{1,0:T(8,128)(2,1)}), bf16[8192,128]{1,0:T(8,128)(2,1)}) %all-gather.50.cloned.1.call-update) | async-done | bytes 2097168 | tf_op jit(solution)/shard_map/all_gather | solution.py:75
  1075.2 14.3 fusion.157
  1114.2 12.9 fusion.173
  1127.1 11.9 reduce-scatter.35.cloned.1.call-done
  1154.3 58.4 %all-gather.36.cloned.1.call-done = bf16[8192,1,128]{0,2,1:T(8,128)(2,1)} async-done(((bf16[128,1,128]{0,2,1:T(8,128)(2,1)}), bf16[8192,1,128]{0,2,1:T(8,128)(2,1)}) %all-gather.36.cloned.1.call-update) | async-done | bytes 2097168 | tf_op jit(solution)/shard_map/all_gather | solution.py:74
  1212.7 12.3 fusion.13
  1235.9 43.7 %all-gather.52.cloned.1.call-done = bf16[8192,128]{1,0:T(8,128)(2,1)} async-done(((bf16[128,128]{1,0:T(8,128)(2,1)}), bf16[8192,128]{1,0:T(8,128)(2,1)}) %all-gather.52.cloned.1.call-update) | async-done | bytes 2097168 | tf_op jit(solution)/shard_map/all_gather | solution.py:75
  1279.6 14.3 fusion.158
  1318.9 12.9 fusion.176
  1331.8 11.9 reduce-scatter.39.cloned.1.call-done
  1358.9 58.5 %all-gather.38.cloned.1.call-done = bf16[8192,1,128]{0,2,1:T(8,128)(2,1)} async-done(((bf16[128,1,128]{0,2,1:T(8,128)(2,1)}), bf16[8192,1,128]{0,2,1:T(8,128)(2,1)}) %all-gather.38.cloned.1.call-update) | async-done | bytes 2097168 | tf_op jit(solution)/shard_map/all_gather | solution.py:74
  1417.4 12.3 fusion.14
  1440.6 43.6 %all-gather.54.cloned.1.call-done = bf16[8192,128]{1,0:T(8,128)(2,1)} async-done(((bf16[128,128]{1,0:T(8,128)(2,1)}), bf16[8192,128]{1,0:T(8,128)(2,1)}) %all-gather.54.cloned.1.call-update) | async-done | bytes 2097168 | tf_op jit(solution)/shard_map/all_gather | solution.py:75
  1484.2 14.3 fusion.159
  1523.2 12.9 fusion.179
  1536.1 11.9 reduce-scatter.43.cloned.1.call-done
  1562.7 58.4 %all-gather.40.cloned.1.call-done = bf16[8192,1,128]{0,2,1:T(8,128)(2,1)} async-done(((bf16[128,1,128]{0,2,1:T(8,128)(2,1)}), bf16[8192,1,128]{0,2,1:T(8,128)(2,1)}) %all-gather.40.cloned.1.call-update) | async-done | bytes 2097168 | tf_op jit(solution)/shard_map/all_gather | solution.py:74
  1621.1 12.3 fusion.15
  1644.3 43.5 %all-gather.56.cloned.1.call-done = bf16[8192,128]{1,0:T(8,128)(2,1)} async-done(((bf16[128,128]{1,0:T(8,128)(2,1)}), bf16[8192,128]{1,0:T(8,128)(2,1)}) %all-gather.56.cloned.1.call-update) | async-done | bytes 2097168 | tf_op jit(solution)/shard_map/all_gather | solution.py:75
  1687.9 14.4 fusion.160
  1726.3 12.8 fusion.182
  (386 shorter events, 434.4 us)
Async XLA Ops:
  7.2 206.5 %all-gather.26.cloned.1.call-start = ((), (), s32[]{:S(2)}) async-start(), calls=%async_computation.16 | async-start | bytes 2129920 | tf_op jit(solution)/shard_map/all_gather | solution.py:74
  21.9 214.4 %all-gather.42.cloned.1.call-start = ((), (), s32[]{:S(2)}) async-start(), calls=%async_computation.40 | async-start | bytes 2129920 | tf_op jit(solution)/shard_map/all_gather | solution.py:75
  23.8 259.1 %reduce-scatter.17.cloned.1.call-start = ((), (), s32[]{:S(2)}) async-start(), calls=%async_computation.17 | async-start | bytes 589824 | tf_op jit(solution)/shard_map/reduce_scatter | solution.py:79
  250.7 70.6 %reduce-scatter.19.cloned.1.call-start = ((), (), s32[]{:S(2)}) async-start(), calls=%async_computation.18 | async-start | bytes 589824 | tf_op jit(solution)/shard_map/reduce_scatter | solution.py:86
  309.4 85.6 %all-gather.28.cloned.1.call-start = ((), (), s32[]{:S(2)}) async-start(), calls=%async_computation.19 | async-start | bytes 2129920 | tf_op jit(solution)/shard_map/all_gather | solution.py:74
  329.1 132.7 %all-gather.44.cloned.1.call-start = ((), (), s32[]{:S(2)}) async-start(), calls=%async_computation.41 | async-start | bytes 2129920 | tf_op jit(solution)/shard_map/all_gather | solution.py:75
  331.1 156.0 %reduce-scatter.21.cloned.1.call-start = ((), (), s32[]{:S(2)}) async-start(), calls=%async_computation.20 | async-start | bytes 589824 | tf_op jit(solution)/shard_map/reduce_scatter | solution.py:79
  476.1 49.7 %reduce-scatter.23.cloned.1.call-start = ((), (), s32[]{:S(2)}) async-start(), calls=%async_computation.21 | async-start | bytes 589824 | tf_op jit(solution)/shard_map/reduce_scatter | solution.py:86
  501.0 26.9 %copy-start.75 = (f32[1536]{0:T(1024)S(1)}, f32[1536]{0:T(1024)}, u32[]{:S(2)}) copy-start(f32[1536]{0:T(1024)} %get-tuple-element.166) | copy-start | bytes 18436
  501.0 34.9 %copy-start.5 = (bf16[768,1536]{0,1:T(8,128)(2,1)S(1)}, bf16[768,1536]{0,1:T(8,128)(2,1)}, u32[]{:S(2)}) copy-start(bf16[768,1536]{0,1:T(8,128)(2,1)} %get-tuple-element.234) | copy-start | bytes 7077892
  513.9 85.6 %all-gather.30.cloned.1.call-start = ((), (), s32[]{:S(2)}) async-start(), calls=%async_computation.22 | async-start | bytes 2129920 | tf_op jit(solution)/shard_map/all_gather | solution.py:74
  533.6 132.7 %all-gather.46.cloned.1.call-start = ((), (), s32[]{:S(2)}) async-start(), calls=%async_computation.42 | async-start | bytes 2129920 | tf_op jit(solution)/shard_map/all_gather | solution.py:75
  535.7 156.1 %reduce-scatter.25.cloned.1.call-start = ((), (), s32[]{:S(2)}) async-start(), calls=%async_computation.23 | async-start | bytes 589824 | tf_op jit(solution)/shard_map/reduce_scatter | solution.py:79
  680.7 49.5 %reduce-scatter.27.cloned.1.call-start = ((), (), s32[]{:S(2)}) async-start(), calls=%async_computation.24 | async-start | bytes 589824 | tf_op jit(solution)/shard_map/reduce_scatter | solution.py:86
  705.3 26.9 %copy-start.74 = (f32[1536]{0:T(1024)S(1)}, f32[1536]{0:T(1024)}, u32[]{:S(2)}) copy-start(f32[1536]{0:T(1024)} %get-tuple-element.165) | copy-start | bytes 18436
  705.3 35.0 %copy-start.4 = (bf16[768,1536]{0,1:T(8,128)(2,1)S(1)}, bf16[768,1536]{0,1:T(8,128)(2,1)}, u32[]{:S(2)}) copy-start(bf16[768,1536]{0,1:T(8,128)(2,1)} %get-tuple-element.224) | copy-start | bytes 7077892
  718.2 85.6 %all-gather.32.cloned.1.call-start = ((), (), s32[]{:S(2)}) async-start(), calls=%async_computation.25 | async-start | bytes 2129920 | tf_op jit(solution)/shard_map/all_gather | solution.py:74
  737.9 132.7 %all-gather.48.cloned.1.call-start = ((), (), s32[]{:S(2)}) async-start(), calls=%async_computation.43 | async-start | bytes 2129920 | tf_op jit(solution)/shard_map/all_gather | solution.py:75
  740.0 156.1 %reduce-scatter.29.cloned.1.call-start = ((), (), s32[]{:S(2)}) async-start(), calls=%async_computation.26 | async-start | bytes 589824 | tf_op jit(solution)/shard_map/reduce_scatter | solution.py:79
  870.6 26.5 %copy-start.68 = (f32[1536]{0:T(1024)S(1)}, f32[1536]{0:T(1024)}, u32[]{:S(2)}) copy-start(f32[1536]{0:T(1024)} %get-tuple-element.182) | copy-start | bytes 18436
  885.0 49.7 %reduce-scatter.31.cloned.1.call-start = ((), (), s32[]{:S(2)}) async-start(), calls=%async_computation.27 | async-start | bytes 589824 | tf_op jit(solution)/shard_map/reduce_scatter | solution.py:86
  909.9 26.9 %copy-start.73 = (f32[1536]{0:T(1024)S(1)}, f32[1536]{0:T(1024)}, u32[]{:S(2)}) copy-start(f32[1536]{0:T(1024)} %get-tuple-element.164) | copy-start | bytes 18436
  909.9 34.9 %copy-start.3 = (bf16[768,1536]{0,1:T(8,128)(2,1)S(1)}, bf16[768,1536]{0,1:T(8,128)(2,1)}, u32[]{:S(2)}) copy-start(bf16[768,1536]{0,1:T(8,128)(2,1)} %get-tuple-element.223) | copy-start | bytes 7077892
  922.8 85.6 %all-gather.34.cloned.1.call-start = ((), (), s32[]{:S(2)}) async-start(), calls=%async_computation.28 | async-start | bytes 2129920 | tf_op jit(solution)/shard_map/all_gather | solution.py:74
  942.5 132.7 %all-gather.50.cloned.1.call-start = ((), (), s32[]{:S(2)}) async-start(), calls=%async_computation.44 | async-start | bytes 2129920 | tf_op jit(solution)/shard_map/all_gather | solution.py:75
  944.5 156.1 %reduce-scatter.33.cloned.1.call-start = ((), (), s32[]{:S(2)}) async-start(), calls=%async_computation.29 | async-start | bytes 589824 | tf_op jit(solution)/shard_map/reduce_scatter | solution.py:79
  1075.2 26.5 %copy-start.67 = (f32[1536]{0:T(1024)S(1)}, f32[1536]{0:T(1024)}, u32[]{:S(2)}) copy-start(f32[1536]{0:T(1024)} %get-tuple-element.181) | copy-start | bytes 18436
  1089.6 49.5 %reduce-scatter.35.cloned.1.call-start = ((), (), s32[]{:S(2)}) async-start(), calls=%async_computation.30 | async-start | bytes 589824 | tf_op jit(solution)/shard_map/reduce_scatter | solution.py:86
  1114.2 26.9 %copy-start.72 = (f32[1536]{0:T(1024)S(1)}, f32[1536]{0:T(1024)}, u32[]{:S(2)}) copy-start(f32[1536]{0:T(1024)} %get-tuple-element.163) | copy-start | bytes 18436
  1114.2 35.0 %copy-start.2 = (bf16[768,1536]{0,1:T(8,128)(2,1)S(1)}, bf16[768,1536]{0,1:T(8,128)(2,1)}, u32[]{:S(2)}) copy-start(bf16[768,1536]{0,1:T(8,128)(2,1)} %get-tuple-element.222) | copy-start | bytes 7077892
  1127.1 85.6 %all-gather.36.cloned.1.call-start = ((), (), s32[]{:S(2)}) async-start(), calls=%async_computation.31 | async-start | bytes 2129920 | tf_op jit(solution)/shard_map/all_gather | solution.py:74
  1146.8 132.9 %all-gather.52.cloned.1.call-start = ((), (), s32[]{:S(2)}) async-start(), calls=%async_computation.45 | async-start | bytes 2129920 | tf_op jit(solution)/shard_map/all_gather | solution.py:75
  1148.8 156.2 %reduce-scatter.37.cloned.1.call-start = ((), (), s32[]{:S(2)}) async-start(), calls=%async_computation.32 | async-start | bytes 589824 | tf_op jit(solution)/shard_map/reduce_scatter | solution.py:79
  1294.0 49.7 %reduce-scatter.39.cloned.1.call-start = ((), (), s32[]{:S(2)}) async-start(), calls=%async_computation.33 | async-start | bytes 589824 | tf_op jit(solution)/shard_map/reduce_scatter | solution.py:86
  1318.9 26.9 %copy-start.71 = (f32[1536]{0:T(1024)S(1)}, f32[1536]{0:T(1024)}, u32[]{:S(2)}) copy-start(f32[1536]{0:T(1024)} %get-tuple-element.169) | copy-start | bytes 18436
  1318.9 34.9 %copy-start.1 = (bf16[768,1536]{0,1:T(8,128)(2,1)S(1)}, bf16[768,1536]{0,1:T(8,128)(2,1)}, u32[]{:S(2)}) copy-start(bf16[768,1536]{0,1:T(8,128)(2,1)} %get-tuple-element.237) | copy-start | bytes 7077892
  1331.8 85.6 %all-gather.38.cloned.1.call-start = ((), (), s32[]{:S(2)}) async-start(), calls=%async_computation.34 | async-start | bytes 2129920 | tf_op jit(solution)/shard_map/all_gather | solution.py:74
  1351.5 132.7 %all-gather.54.cloned.1.call-start = ((), (), s32[]{:S(2)}) async-start(), calls=%async_computation.46 | async-start | bytes 2129920 | tf_op jit(solution)/shard_map/all_gather | solution.py:75
  1353.5 156.1 %reduce-scatter.41.cloned.1.call-start = ((), (), s32[]{:S(2)}) async-start(), calls=%async_computation.35 | async-start | bytes 589824 | tf_op jit(solution)/shard_map/reduce_scatter | solution.py:79
  1484.2 26.5 %copy-start.65 = (f32[1536]{0:T(1024)S(1)}, f32[1536]{0:T(1024)}, u32[]{:S(2)}) copy-start(f32[1536]{0:T(1024)} %get-tuple-element.186) | copy-start | bytes 18436
  1498.6 49.5 %reduce-scatter.43.cloned.1.call-start = ((), (), s32[]{:S(2)}) async-start(), calls=%async_computation.36 | async-start | bytes 589824 | tf_op jit(solution)/shard_map/reduce_scatter | solution.py:86
  1523.2 26.9 %copy-start.70 = (f32[1536]{0:T(1024)S(1)}, f32[1536]{0:T(1024)}, u32[]{:S(2)}) copy-start(f32[1536]{0:T(1024)} %get-tuple-element.162) | copy-start | bytes 18436
  1523.2 34.4 %copy-start = (bf16[768,1536]{0,1:T(8,128)(2,1)S(1)}, bf16[768,1536]{0,1:T(8,128)(2,1)}, u32[]{:S(2)}) copy-start(bf16[768,1536]{0,1:T(8,128)(2,1)} %get-tuple-element.221) | copy-start | bytes 7077892
  1536.1 85.0 %all-gather.40.cloned.1.call-start = ((), (), s32[]{:S(2)}) async-start(), calls=%async_computation.37 | async-start | bytes 2129920 | tf_op jit(solution)/shard_map/all_gather | solution.py:74
  1555.2 132.7 %all-gather.56.cloned.1.call-start = ((), (), s32[]{:S(2)}) async-start(), calls=%async_computation.47 | async-start | bytes 2129920 | tf_op jit(solution)/shard_map/all_gather | solution.py:75
  1557.2 156.1 %reduce-scatter.45.cloned.1.call-start = ((), (), s32[]{:S(2)}) async-start(), calls=%async_computation.38 | async-start | bytes 589824 | tf_op jit(solution)/shard_map/reduce_scatter | solution.py:79
  1687.9 26.6 %copy-start.64 = (f32[1536]{0:T(1024)S(1)}, f32[1536]{0:T(1024)}, u32[]{:S(2)}) copy-start(f32[1536]{0:T(1024)} %get-tuple-element.185) | copy-start | bytes 18436
  1702.3 48.8 %reduce-scatter.47.cloned.1.call-start = ((), (), s32[]{:S(2)}) async-start(), calls=%async_computation.39 | async-start | bytes 589824 | tf_op jit(solution)/shard_map/reduce_scatter | solution.py:86
  (60 other events, 508.3 us)
Sparse Core Ops, SparseCore 0:
  22.0 67.0 all-gather.25
  92.0 63.4 all-gather.41
  250.8 32.0 reduce-scatter.16
  309.5 11.7 reduce-scatter.18
  329.2 65.7 all-gather.27
  398.3 63.4 all-gather.43
  476.2 10.8 reduce-scatter.20
  514.0 11.7 reduce-scatter.22
  533.7 65.7 all-gather.29
  602.8 63.4 all-gather.45
  680.8 10.8 reduce-scatter.24
  718.3 11.7 reduce-scatter.26
  738.0 65.7 all-gather.31
  807.1 63.4 all-gather.47
  885.1 10.8 reduce-scatter.28
  922.9 11.7 reduce-scatter.30
  942.6 65.7 all-gather.33
  1011.7 63.4 all-gather.49
  1089.7 10.8 reduce-scatter.32
  1127.2 11.7 reduce-scatter.34
  1146.9 65.7 all-gather.35
  1216.1 63.4 all-gather.51
  1294.1 10.8 reduce-scatter.36
  1331.9 11.7 reduce-scatter.38
  1351.6 65.7 all-gather.37
  1420.7 63.4 all-gather.53
  1498.7 10.8 reduce-scatter.40
  1536.2 11.7 reduce-scatter.42
  1555.3 65.7 all-gather.39
  1624.4 63.4 all-gather.55
  1702.4 10.8 reduce-scatter.44
  1739.2 11.7 reduce-scatter.46
where the time goes:
time: 1770 us; the launch traced here: 1760 us
  waiting for transfers between devices  918 us (52%)
  matrix products  429 us (24%)
  blocking collectives  189 us (11%)
  other arithmetic  134 us (8%)
  local copies, waits for them, and re-layouts  70.4 us (4%)
    all_gather x8, waiting for transfers between devices, device_fn(): k_keys = lax.all_gather(k_rows, 'sp', axis=0, tiled=True)  409 us
    all_gather x8, waiting for transfers between devices, device_fn(): v_keys = lax.all_gather(v_rows, 'sp', axis=0, tiled=True)  305 us
    all_gather x1, blocking collectives, device_fn(): key_seg = lax.all_gather(row_seg, 'sp', tiled=True)  151 us
    dot_general x8, matrix products, device_fn(): jnp.einsum('nkgqd,kgdm->nqm', att_out, wo_heads, preferred_element_type=j...  115 us
    reduce_scatter x8, waiting for transfers between devices, device_fn(): attn_res = lax.psum_scatter(part_sum, 'tp', scatter_dimension=0, tiled=True)  109 us
    dot_general x8, matrix products, device_fn(): jnp.dot(act_vals, w_down[layer_idx], preferred_element_type=jnp.float32)  103 us
    dot_general x8, matrix products, one_block(): jnp.einsum('qkgd,skd->kgqs', q_blk, k_keys, preferred_element_type=jnp.fl...  97.5 us
    reduce_scatter x8, waiting for transfers between devices, device_fn(): mlp_res = lax.psum_scatter(down_part, 'tp', scatter_dimension=0, tiled=True)  94.2 us
  transfers between devices with their start and end apart: 32, of which 30 were waited for; matrix products, arithmetic and copies ran while one was open for 16% of the time, Pallas kernels for 0%

commit v1 on v0

v1 whole, which is shorter than its diff:
```python
import math
import jax
import jax.numpy as jnp
from jax import lax
from jax.experimental import pallas as pl
from jax.experimental.pallas import tpu as pltpu
from jax.sharding import PartitionSpec as P

HEAD_DIM = 128
ROPE_BASE = 1e4
NORM_EPS = 1e-5
SCORE_SCALE = HEAD_DIM ** -0.5
EXP_SCALE = SCORE_SCALE * math.log2(math.e)
BIG = 1e30
MESH = pl.DeviceIdType.MESH
F32 = jnp.float32
BF16 = jnp.bfloat16

PART_ROWS = (48, 48, 32)
PART_OFF = (0, 48, 96)
PART_STRIDES = ((1, 4, 16), (4, 16, 1), (16, 1, 4))
N_SEM = 23


def rms_rows(x_val, gain_row):
    x32 = x_val.astype(F32)
    inv_rms = lax.rsqrt(jnp.mean(x32 * x32, axis=-1, keepdims=True) + NORM_EPS)
    return (x32 * inv_rms * gain_row).astype(BF16)


def stack_kernel(n_layers, rows, half_rows, hid_ref, aux_ref, ga_ref, gm_ref, wq_h, wk_h, wv_h, wo_h, wg_h, wu_h, wd_h,
                 hid_out, k_out, v_out,
                 x_buf, aux_buf, cnt_buf, wqkv, wo, wg, wu, wd, kv0, kv1, kv2, ext0, ext1, ext2, q_t, mask_add,
                 m_s, l_s, acc_s, n_s, o_s, act_s, kst, vst, snd_a, rcv_a, snd_b, rcv_b,
                 ini_ss, ini_rs, cnt_ss, cnt_rs, w_sem, g_ss, g_rs, x_ss, x_rs, c_sem):
    sp = lax.axis_index('sp')
    tp = lax.axis_index('tp')
    kvs = (kv0, kv1, kv2)
    exts = (ext0, ext1, ext2)
    n_q = wq_h.shape[2]
    n_heads = n_q // HEAD_DIM
    d_model = hid_ref.shape[1]
    ffn = wg_h.shape[2]

    def coord(stride):
        return (sp // stride) % 4

    def neighbour(stride, delta):
        here = coord(stride)
        return sp + ((here + delta) % 4 - here) * stride

    def remote(src, dst, ss, rs, sp_to, tp_to):
        return pltpu.make_async_remote_copy(src_ref=src, dst_ref=dst, send_sem=ss, recv_sem=rs,
                                            device_id={'sp': sp_to, 'tp': tp_to}, device_id_type=MESH)

    n_split = 4
    gr = d_model // n_split
    dr = ffn // n_split

    def qkv_copies(layer):
        nk = wk_h.shape[2]
        return [pltpu.make_async_copy(wq_h.at[layer], wqkv.at[:, 0:n_q], w_sem.at[0]),
                pltpu.make_async_copy(wk_h.at[layer], wqkv.at[:, n_q:n_q + nk], w_sem.at[1]),
                pltpu.make_async_copy(wv_h.at[layer], wqkv.at[:, n_q + nk:n_q + 2 * nk], w_sem.at[2])]

    def wo_copies(layer):
        return [pltpu.make_async_copy(wo_h.at[layer], wo, w_sem.at[3])]

    def gu_copies(layer):
        out = []
        for c in range(n_split):
            r = pl.ds(c * gr, gr)
            out.append(pltpu.make_async_copy(wg_h.at[layer, r], wg.at[r], w_sem.at[4 + c]))
            out.append(pltpu.make_async_copy(wu_h.at[layer, r], wu.at[r], w_sem.at[4 + n_split + c]))
        return out

    def down_copies(layer):
        out = []
        for c in range(n_split):
            r = pl.ds(c * dr, dr)
            out.append(pltpu.make_async_copy(wd_h.at[layer, r], wd.at[r], w_sem.at[4 + 2 * n_split + c]))
        return out

    def start_all(copies):
        for c in copies:
            c.start()

    def wait_all(copies):
        for c in copies:
            c.wait()

    start_all(qkv_copies(0))
    start_all(wo_copies(0))
    start_all(gu_copies(0))
    start_all(down_copies(0))

    barrier = pltpu.get_barrier_semaphore()
    for stride in (1, 4, 16):
        for delta in (1, 2, 3):
            pl.semaphore_signal(barrier, inc=1, device_id={'sp': neighbour(stride, delta), 'tp': tp}, device_id_type=MESH)
    pl.semaphore_signal(barrier, inc=1, device_id={'sp': sp, 'tp': 1 - tp}, device_id_type=MESH)
    pl.semaphore_wait(barrier, 10)

    mine = pl.ds(pl.multiple_of(tp * half_rows, half_rows), half_rows)
    theirs = pl.ds(pl.multiple_of((1 - tp) * half_rows, half_rows), half_rows)
    swaps = [remote(hid_ref, x_buf.at[mine], ini_ss.at[0], ini_rs.at[0], sp, 1 - tp),
             remote(aux_ref, aux_buf.at[:, mine], ini_ss.at[1], ini_rs.at[1], sp, 1 - tp)]
    start_all(swaps)
    x_buf[mine, :] = hid_ref[...]
    for a in range(3):
        aux_buf[a, mine, :] = aux_ref[a]
    for s in swaps:
        s.wait_send()
    remote(hid_ref, x_buf.at[theirs], ini_ss.at[0], ini_rs.at[0], sp, 1 - tp).wait_recv()
    remote(aux_ref, aux_buf.at[:, theirs], ini_ss.at[1], ini_rs.at[1], sp, 1 - tp).wait_recv()

    seg_col = aux_buf[2]
    lane_f = lax.broadcasted_iota(jnp.int32, (rows, 128), 1).astype(F32)
    below = jnp.sum(jnp.where(seg_col < lane_f, 1.0, 0.0), axis=0, keepdims=True)
    upto = jnp.sum(jnp.where(seg_col < lane_f + 1.0, 1.0, 0.0), axis=0, keepdims=True)
    mx, my, mz = coord(1), coord(4), coord(16)
    cnt_buf[mz, my, mx] = jnp.concatenate([jnp.broadcast_to(below, (8, 128)), jnp.broadcast_to(upto, (8, 128))], axis=0)
    for phase, stride in enumerate((1, 4, 16)):
        def block(cz, cy, cx):
            return (cnt_buf.at[cz, cy, cx], cnt_buf.at[cz, cy], cnt_buf.at[cz])[phase]
        for delta in (1, 2, 3):
            b = block(mz, my, mx)
            i = phase * 3 + delta - 1
            remote(b, b, cnt_ss.at[i], cnt_rs.at[i], neighbour(stride, delta), tp).start()
        for delta in (1, 2, 3):
            i = phase * 3 + delta - 1
            frm = [mz, my, mx]
            frm[2 - phase] = (frm[2 - phase] - delta) % 4
            b = block(*frm)
            c = remote(b, b, cnt_ss.at[i], cnt_rs.at[i], neighbour(stride, delta), tp)
            c.wait_send()
            c.wait_recv()
    total = jnp.sum(cnt_buf[...].reshape(64, 16, 128), axis=0)
    seg_lo = total[0:1, :]
    seg_hi = total[8:9, :]

    for p in range(3):
        s1, s2, s3 = PART_STRIDES[p]
        pr = PART_ROWS[p]
        row_i = lax.broadcasted_iota(jnp.int32, (pr, 128), 0)
        lane_i = lax.broadcasted_iota(jnp.int32, (pr, 128), 1)

        def fill(b, carry, p=p, s1=s1, s2=s2, s3=s3, pr=pr, row_i=row_i, lane_i=lane_i):
            c3 = b // 16
            c2 = (b // 4) % 4
            c1 = b % 4
            blk = c3 * s3 + c2 * s2 + c1 * s1
            idx = (row_i + (blk * rows + PART_OFF[p])).astype(F32)
            one_hot = jnp.where(idx >= seg_lo, 1.0, 0.0) * jnp.where(idx < seg_hi, 1.0, 0.0)
            late = jnp.where(row_i * 0 + blk >= sp, 1.0, 0.0)
            val = jnp.where(lane_i < 4, one_hot, jnp.where(lane_i == 4, late, 0.0))
            exts[p][c3, c2, c1] = val.astype(BF16)
            return carry
        lax.fori_loop(0, 64, fill, 0)

    seg_row = jnp.transpose(seg_col)
    row_i = lax.broadcasted_iota(jnp.int32, (rows, 128), 0)
    col_i = lax.broadcasted_iota(jnp.int32, (rows, 128), 1)
    q_side = jnp.where(row_i < 4, jnp.where(seg_row == row_i.astype(F32), 0.0, -BIG), jnp.where(row_i == 4, -BIG, 0.0)).astype(BF16)
    for h in range(n_heads):
        q_t[128:256, h * 128:(h + 1) * 128] = q_side
    mask_add[...] = jnp.where(row_i <= col_i, jnp.where(seg_col == seg_row, 0.0, -BIG), -BIG)

    def soft_step(keys, vals, cols, add, first):
        n_c = cols.stop - cols.start
        q_rows = slice(0, keys.shape[1])
        s = jnp.dot(keys, q_t[q_rows, cols], preferred_element_type=F32)
        if add is not None:
            s = s + add
        top = jnp.max(s, axis=0, keepdims=True)
        if first:
            m_new = top
        else:
            m_old = m_s[0:1, cols]
            m_new = jnp.maximum(m_old, top)
        e = jnp.exp2((s - m_new) * EXP_SCALE)
        e_sum = jnp.sum(e, axis=0, keepdims=True)
        pv = lax.dot_general(vals, e.astype(BF16), (((0,), (0,)), ((), ())), preferred_element_type=F32)
        if first:
            l_new = e_sum
            acc_s[:, cols] = pv
        else:
            alpha = jnp.exp2((m_old - m_new) * EXP_SCALE)
            l_new = l_s[0:1, cols] * alpha + e_sum
            acc_s[:, cols] = acc_s[:, cols] * alpha + pv
        m_s[:, cols] = jnp.broadcast_to(m_new, (8, n_c))
        l_s[:, cols] = jnp.broadcast_to(l_new, (8, n_c))

    col_tiles = [slice(c, c + 256) for c in range(0, n_q, 256)]

    def plane_step(p, par, c3):
        n_k = 16 * PART_ROWS[p]
        kv = kvs[p][par, c3].reshape(n_k, 256)
        keys = jnp.concatenate([kv[:, 0:128], exts[p][c3].reshape(n_k, 128)], axis=1)
        for cols in col_tiles:
            soft_step(keys, kv[:, 128:256], cols, None, False)

    def layer_step(layer, carry):
        par = layer % 2
        has_next = layer + 1 < n_layers

        def send(p, i, ref, stride, delta):
            remote(ref, ref, g_ss.at[p, i], g_rs.at[par, p, i], neighbour(stride, delta), tp).start()

        def got(p, i, ref):
            remote(ref, ref, g_ss.at[p, i], g_rs.at[par, p, i], sp, 1 - tp).wait_recv()

        def sent(p, i, ref):
            remote(ref, ref, g_ss.at[p, i], g_rs.at[par, p, i], sp, 1 - tp).wait_send()

        coords = [tuple(coord(s) for s in PART_STRIDES[p]) for p in range(3)]

        n_s[...] = rms_rows(x_buf[...], ga_ref[layer])
        wait_all(qkv_copies(layer))
        cos_t = aux_buf[0]
        sin_t = aux_buf[1]

        def rope(v):
            return (v * cos_t + pltpu.roll(v, HEAD_DIM // 2, 1) * sin_t).astype(BF16)

        kv_lin = jnp.dot(n_s[...], wqkv[:, n_q:], preferred_element_type=F32)
        k_rot = rope(kv_lin[:, 0:128])
        v_val = kv_lin[:, 128:256].astype(BF16)
        kst[...] = k_rot
        vst[...] = v_val
        kv_val = jnp.concatenate([k_rot, v_val], axis=1)
        for p in range(3):
            m1, m2, m3 = coords[p]
            kvs[p][par, m3, m2, m1] = kv_val[PART_OFF[p]:PART_OFF[p] + PART_ROWS[p], :]
        cache = [pltpu.make_async_copy(kst, k_out.at[layer], c_sem.at[0]),
                 pltpu.make_async_copy(vst, v_out.at[layer], c_sem.at[1])]
        start_all(cache)
        for p in range(3):
            m1, m2, m3 = coords[p]
            own = kvs[p].at[par, m3, m2, m1]
            for i, delta in enumerate((1, 3, 2)):
                send(p, i, own, PART_STRIDES[p][0], delta)
        q_lin = jnp.dot(n_s[...], wqkv[:, 0:n_q], preferred_element_type=F32)
        for h in range(n_heads):
            q_h = rope(q_lin[:, h * 128:(h + 1) * 128])
            q_t[0:128, h * 128:(h + 1) * 128] = jnp.transpose(q_h)

        @pl.when(has_next)
        def _():
            start_all(qkv_copies(layer + 1))

        mask2 = jnp.concatenate([mask_add[...], mask_add[...]], axis=1)
        for cols in col_tiles:
            soft_step(kst[...], vst[...], cols, mask2, True)

        for p in range(3):
            m1, m2, m3 = coords[p]
            s1, s2, s3 = PART_STRIDES[p]
            for i, delta in enumerate((1, 3, 2)):
                got(p, i, kvs[p].at[par, m3, m2, (m1 - delta) % 4])
            row = kvs[p].at[par, m3, m2]
            send(p, 3, row, s2, 1)
            send(p, 4, row, s2, 3)
            send(p, 7, row, s3, 1)
            send(p, 8, row, s3, 3)

        def pass_on3(p, r, c2):
            m1, m2, m3 = coords[p]
            s3 = PART_STRIDES[p][2]
            lo = (m3 - 1) % 4
            hi = (m3 + 1) % 4
            got(p, 7 + 4 * r, kvs[p].at[par, lo, c2])
            send(p, 9 + 4 * r, kvs[p].at[par, lo, c2, 0:2], s3, 1)
            got(p, 8 + 4 * r, kvs[p].at[par, hi, c2])
            send(p, 10 + 4 * r, kvs[p].at[par, hi, c2, 2:4], s3, 3)

        for p in range(3):
            m1, m2, m3 = coords[p]
            s1, s2, s3 = PART_STRIDES[p]
            lo = (m2 - 1) % 4
            hi = (m2 + 1) % 4
            got(p, 3, kvs[p].at[par, m3, lo])
            send(p, 5, kvs[p].at[par, m3, lo, 0:2], s2, 1)
            send(p, 11, kvs[p].at[par, m3, lo], s3, 1)
            send(p, 12, kvs[p].at[par, m3, lo], s3, 3)
            got(p, 4, kvs[p].at[par, m3, hi])
            send(p, 6, kvs[p].at[par, m3, hi, 2:4], s2, 3)
            send(p, 15, kvs[p].at[par, m3, hi], s3, 1)
            send(p, 16, kvs[p].at[par, m3, hi], s3, 3)
        for p in range(3):
            pass_on3(p, 0, coords[p][1])
        for p in range(3):
            m1, m2, m3 = coords[p]
            s1, s2, s3 = PART_STRIDES[p]
            far = (m2 + 2) % 4
            got(p, 5, kvs[p].at[par, m3, far, 0:2])
            got(p, 6, kvs[p].at[par, m3, far, 2:4])
            send(p, 19, kvs[p].at[par, m3, far], s3, 1)
            send(p, 20, kvs[p].at[par, m3, far], s3, 3)
        for p in range(3):
            plane_step(p, par, coords[p][2])
        for r, off in ((1, 3), (2, 1), (3, 2)):
            for p in range(3):
                pass_on3(p, r, (coords[p][1] + off) % 4)
        for p in range(3):
            plane_step(p, par, (coords[p][2] + 3) % 4)
        for p in range(3):
            plane_step(p, par, (coords[p][2] + 1) % 4)
        for p in range(3):
            m1, m2, m3 = coords[p]
            far = (m3 + 2) % 4
            for r, off in ((0, 0), (1, 3), (2, 1), (3, 2)):
                c2 = (m2 + off) % 4
                got(p, 9 + 4 * r, kvs[p].at[par, far, c2, 0:2])
                got(p, 10 + 4 * r, kvs[p].at[par, far, c2, 2:4])
            plane_step(p, par, far)

        for h in range(n_heads):
            cols = slice(h * 128, (h + 1) * 128)
            o_t = acc_s[:, cols] * (1.0 / l_s[0:1, cols])
            o_s[:, cols] = jnp.transpose(o_t.astype(BF16))
        wait_all(wo_copies(layer))
        n_t = snd_a.shape[0]
        tw = snd_a.shape[2]
        swap_a = [remote(snd_a.at[t], rcv_a.at[t], x_ss.at[0, t], x_rs.at[0, t], sp, 1 - tp) for t in range(n_t)]
        swap_b = [remote(snd_b.at[t], rcv_b.at[t], x_ss.at[1, t], x_rs.at[1, t], sp, 1 - tp) for t in range(n_t)]
        for t in range(n_t):
            part = jnp.dot(o_s[...], wo[:, t * tw:(t + 1) * tw], preferred_element_type=F32)
            snd_a[t] = part.astype(BF16)
            swap_a[t].start()

        for p in range(3):
            m1, m2, m3 = coords[p]
            for i in range(3):
                sent(p, i, kvs[p].at[par, m3, m2, m1])
            for i in (3, 4):
                sent(p, i, kvs[p].at[par, m3, m2])
            for i in (5, 6):
                sent(p, i, kvs[p].at[par, m3, m2, 0:2])
            for r in range(4):
                for i in (7, 8):
                    sent(p, i + 4 * r, kvs[p].at[par, m3, m2])
                for i in (9, 10):
                    sent(p, i + 4 * r, kvs[p].at[par, m3, m2, 0:2])

        @pl.when(has_next)
        def _():
            start_all(wo_copies(layer + 1))

        for t in range(n_t):
            swap_a[t].wait()
            cols = slice(t * tw, (t + 1) * tw)
            res = (snd_a[t].astype(F32) + rcv_a[t].astype(F32)).astype(BF16)
            x_buf[:, cols] = (x_buf[:, cols].astype(F32) + res.astype(F32)).astype(BF16)

        n_s[...] = rms_rows(x_buf[...], gm_ref[layer])
        wait_all(gu_copies(layer))

        def gate_up(cols):
            gate = jnp.dot(n_s[...], wg[:, cols], preferred_element_type=F32)
            up = jnp.dot(n_s[...], wu[:, cols], preferred_element_type=F32)
            act_s[:, cols] = (gate * jax.nn.sigmoid(gate) * up).astype(BF16)

        gt = 1024

        def gate_up_tile(t, c):
            gate_up(pl.ds(pl.multiple_of(t * gt, gt), gt))
            return c
        n_full = ffn // gt
        lax.fori_loop(0, n_full, gate_up_tile, 0)
        if ffn % gt:
            gate_up(slice(n_full * gt, ffn))

        @pl.when(has_next)
        def _():
            start_all(gu_copies(layer + 1))

        wait_all(down_copies(layer))
        for t in range(n_t):
            part = jnp.dot(act_s[...], wd[:, t * tw:(t + 1) * tw], preferred_element_type=F32)
            snd_b[t] = part.astype(BF16)
            swap_b[t].start()

        @pl.when(has_next)
        def _():
            start_all(down_copies(layer + 1))

        wait_all(cache)
        for t in range(n_t):
            swap_b[t].wait()
            cols = slice(t * tw, (t + 1) * tw)
            res = (snd_b[t].astype(F32) + rcv_b[t].astype(F32)).astype(BF16)
            x_buf[:, cols] = (x_buf[:, cols].astype(F32) + res.astype(F32)).astype(BF16)
        return carry

    lax.fori_loop(0, n_layers, layer_step, 0)
    hid_out[...] = x_buf[mine, :]


def solution(mesh):
    tok_spec = P(('dp', 'sp', 'tp'))
    col_spec = P(None, None, 'tp')
    row_spec = P(None, 'tp', None)
    cache_spec = P(None, ('dp', 'sp'), 'tp', None)

    def device_fn(hidden_in, segment_ids, positions, attn_gain, w_q, w_k, w_v, w_o, mlp_gain, w_gate, w_up, w_down):
        half_rows, d_model = hidden_in.shape
        rows = 2 * half_rows
        n_layers, _, n_q = w_q.shape
        ffn = w_gate.shape[2]
        half_dim = HEAD_DIM // 2
        inv_freq = ROPE_BASE ** (-jnp.arange(half_dim, dtype=F32) / half_dim)
        angles = positions.astype(F32)[:, None] * inv_freq
        cos_val = jnp.cos(angles)
        sin_val = jnp.sin(angles)
        aux = jnp.stack([jnp.concatenate([cos_val, cos_val], axis=1), jnp.concatenate([-sin_val, sin_val], axis=1),
                         jnp.broadcast_to(segment_ids.astype(F32)[:, None], (half_rows, HEAD_DIM))])
        vm = pl.BlockSpec(memory_space=pltpu.VMEM)
        anyspec = pl.BlockSpec(memory_space=pl.ANY)
        n_t, tw = 3, d_model // 3
        dma = pltpu.SemaphoreType.DMA
        body = lambda *refs: stack_kernel(n_layers, rows, half_rows, *refs)
        hid, k_c, v_c = pl.pallas_call(
            body,
            out_shape=(jax.ShapeDtypeStruct((half_rows, d_model), BF16),
                       jax.ShapeDtypeStruct((n_layers, rows, HEAD_DIM), BF16),
                       jax.ShapeDtypeStruct((n_layers, rows, HEAD_DIM), BF16)),
            in_specs=[vm, vm, vm, vm] + [anyspec] * 7,
            out_specs=(vm, anyspec, anyspec),
            scratch_shapes=[
                pltpu.VMEM((rows, d_model), BF16),
                pltpu.VMEM((3, rows, 128), F32),
                pltpu.VMEM((4, 4, 4, 16, 128), F32),
                pltpu.VMEM((d_model, n_q + 2 * HEAD_DIM), BF16),
                pltpu.VMEM((n_q, d_model), BF16),
                pltpu.VMEM((d_model, ffn), BF16),
                pltpu.VMEM((d_model, ffn), BF16),
                pltpu.VMEM((ffn, d_model), BF16),
                pltpu.VMEM((2, 4, 4, 4, PART_ROWS[0], 256), BF16),
                pltpu.VMEM((2, 4, 4, 4, PART_ROWS[1], 256), BF16),
                pltpu.VMEM((2, 4, 4, 4, PART_ROWS[2], 256), BF16),
                pltpu.VMEM((4, 4, 4, PART_ROWS[0], 128), BF16),
                pltpu.VMEM((4, 4, 4, PART_ROWS[1], 128), BF16),
                pltpu.VMEM((4, 4, 4, PART_ROWS[2], 128), BF16),
                pltpu.VMEM((256, n_q), BF16),
                pltpu.VMEM((rows, 128), F32),
                pltpu.VMEM((8, n_q), F32),
                pltpu.VMEM((8, n_q), F32),
                pltpu.VMEM((HEAD_DIM, n_q), F32),
                pltpu.VMEM((rows, d_model), BF16),
                pltpu.VMEM((rows, n_q), BF16),
                pltpu.VMEM((rows, ffn), BF16),
                pltpu.VMEM((rows, HEAD_DIM), BF16),
                pltpu.VMEM((rows, HEAD_DIM), BF16),
                pltpu.VMEM((n_t, rows, tw), BF16),
                pltpu.VMEM((n_t, rows, tw), BF16),
                pltpu.VMEM((n_t, rows, tw), BF16),
                pltpu.VMEM((n_t, rows, tw), BF16),
                dma((2,)), dma((2,)), dma((9,)), dma((9,)), dma((16,)),
                dma((3, N_SEM)), dma((2, 3, N_SEM)), dma((2, n_t)), dma((2, n_t)), dma((2,)),
            ],
            compiler_params=pltpu.CompilerParams(collective_id=0, has_side_effects=True, vmem_limit_bytes=67043328),
        )(hidden_in, aux, attn_gain.astype(F32)[:, None, :], mlp_gain.astype(F32)[:, None, :], w_q, w_k, w_v, w_o, w_gate, w_up, w_down)
        return hid, k_c.reshape(n_layers, rows, 1, HEAD_DIM), v_c.reshape(n_layers, rows, 1, HEAD_DIM)

    return jax.shard_map(device_fn, mesh=mesh,
                         in_specs=(P(('dp', 'sp', 'tp'), None), tok_spec, tok_spec, P(), col_spec, col_spec, col_spec, row_spec, P(), col_spec, col_spec, row_spec),
                         out_specs=(P(('dp', 'sp', 'tp'), None), cache_spec, cache_spec), check_vma=False)
```

time: 1770 us -> 413 us (0.23)
  waiting for transfers between devices: 918 us -> 0 us
  matrix products: 429 us -> 0 us
  Pallas kernels: 0 us -> 402 us
  blocking collectives: 189 us -> 0 us
  other arithmetic: 134 us -> 2.25 us
  local copies, waits for them, and re-layouts: 70.4 us -> 7.8 us
    all_gather x16 -> x0, waiting for transfers between devices: 714 us -> none  [the longest x8 409 us: device_fn(): k_keys = lax.all_gather(k_rows, 'sp', axis=0, tiled=True)]
    dot_general x56 -> x0, matrix products: 429 us -> none  [the longest x8 115 us: device_fn(): jnp.einsum('nkgqd,kgdm->nqm', att_out, wo_heads, preferred_element_type=j...]
    pallas_call x0 -> x1, Pallas kernels: none -> 402 us  [device_fn(): pl.pallas_call(body, out_shape=(jax.ShapeDtypeStruct((half_rows, d_model)...]
    reduce_scatter x16 -> x0, waiting for transfers between devices: 203 us -> none  [the longest x8 109 us: device_fn(): attn_res = lax.psum_scatter(part_sum, 'tp', scatter_dimension=0, tiled=True)]
    all_gather x17 -> x0, blocking collectives: 186 us -> none  [the longest x1 151 us: device_fn(): key_seg = lax.all_gather(row_seg, 'sp', tiled=True)]
    reduce_sum x24 -> x0, other arithmetic: 107 us -> none  [the longest x8 87.7 us: one_block(): jax.nn.softmax(jnp.where(allowed, scores, -1e+30), axis=-1)]
    dot_general x9 -> x0, local copies, waits for them, and re-layouts: 34.3 us -> none  [device_fn(): jnp.dot(normed, w_q[layer_idx], preferred_element_type=jnp.float32)]
    unnamed x158 -> x3, local copies, waits for them, and re-layouts: 22.8 us -> 4.96 us
  transfers between devices with their start and end apart: 32 -> 0, of which waited for: 30 -> 0; matrix products, arithmetic and copies ran while one was open for 16% -> 0% of each run, Pallas kernels for 0% -> 0%
where the time goes in v1:
time: 413 us
  Pallas kernels  402 us (97%)
  local copies, waits for them, and re-layouts  7.8 us (2%)
    pallas_call x1, Pallas kernels, device_fn(): pl.pallas_call(body, out_shape=(jax.ShapeDtypeStruct((half_rows, d_model)...  402 us

profile of v1, /device:TPU:1, one launch (start us, length us, event | category | flops | bytes accessed | tf_op | source)
XLA Modules:
  0.0 412.9 jit_solution(2402925311191335627)
XLA Ops:
  0.6 0.7 convert_element_type.9
  1.3 0.7 convert_element_type.8
  2.0 0.1 stack_broadcast_in_dim.2
  2.0 1.4 reshape.21.refs_2_
  3.4 1.4 reshape.22.refs_3_
  4.8 0.2 multiply_cosine_fusion
  5.0 0.1 maximum_bitcast_fusion
  5.1 0.6 pad_maximum_fusion.refs_1_
  5.7 402.2 %shard_map.139 = (bf16[64,1536]{1,0:T(8,128)(2,1)}, bf16[8,128,128]{2,1,0:T(8,128)(2,1)}, bf16[8,128,128]{2,1,0:T(8,128)(2,1)}) custom-call(bf16[64,1536]{1,0:T(8,128)(2,1)} %refs_0_.1, f32[3,64,128]{2,1,0:T(8,128)} %pad_maximum_fusion.refs_1_, f32[8,1,1536]{2,1,0:T(1,128)} %reshape.21.refs_2_, f32[8,1,1536]{2,1,0:T(1,128)} %reshape.22.refs_3_, ...), custom_call_target="tpu_custom_call" | custom-call | tf_op jit(solution)/shard_map/pallas_call | solution.py:423
  407.9 1.6 copy.20
  409.6 1.7 copy.21
  411.2 1.7 copy.22
  (1 shorter events, 0.0 us)

commit v2 on v1

--- a/solution.py
+++ b/solution.py
@@ -18,8 +18,13 @@
 
 PART_ROWS = (48, 48, 32)
 PART_OFF = (0, 48, 96)
-PART_STRIDES = ((1, 4, 16), (4, 16, 1), (16, 1, 4))
+X, Y, Z = range(3)
+AXIS_STRIDE = (1, 4, 16)
+PART_AXES = (((X, Y, Z), (Y, Z, X), (X, Z, Y)), ((Z, Y, X), (X, Z, Y), (X, Y, Z)))
 N_SEM = 23
+OWN, NEXT, FAR, PREV = range(4)
+RING = 4
+LANES = 128
 
 
 def rms_rows(x_val, gain_row):
@@ -32,7 +37,7 @@
                  hid_out, k_out, v_out,
                  x_buf, aux_buf, cnt_buf, wqkv, wo, wg, wu, wd, kv0, kv1, kv2, ext0, ext1, ext2, q_t, mask_add,
                  m_s, l_s, acc_s, n_s, o_s, act_s, kst, vst, snd_a, rcv_a, snd_b, rcv_b,
-                 ini_ss, ini_rs, cnt_ss, cnt_rs, w_sem, g_ss, g_rs, x_ss, x_rs, c_sem):
+                 gain_s, ini_ss, ini_rs, cnt_ss, cnt_rs, w_sem, g_ss, g_rs, x_ss, x_rs, c_sem):
     sp = lax.axis_index('sp')
     tp = lax.axis_index('tp')
     kvs = (kv0, kv1, kv2)
@@ -42,12 +47,18 @@
     d_model = hid_ref.shape[1]
     ffn = wg_h.shape[2]
 
-    def coord(stride):
-        return (sp // stride) % 4
-
-    def neighbour(stride, delta):
-        here = coord(stride)
-        return sp + ((here + delta) % 4 - here) * stride
+    axis_at = [(sp // stride) % RING for stride in AXIS_STRIDE]
+
+    def by_core(pair):
+        return pair[0] + (pair[1] - pair[0]) * tp
+
+    ways = [[(by_core([AXIS_STRIDE[PART_AXES[core][p][d]] for core in range(2)]),
+              by_core([axis_at[PART_AXES[core][p][d]] for core in range(2)])) for d in range(3)] for p in range(3)]
+    coords = [tuple(at for _, at in way) for way in ways]
+
+    def ring_to(way, delta):
+        stride, here = way
+        return sp + ((here + delta) % RING - here) * stride
 
     def remote(src, dst, ss, rs, sp_to, tp_to):
         return pltpu.make_async_remote_copy(src_ref=src, dst_ref=dst, send_sem=ss, recv_sem=rs,
@@ -94,10 +105,13 @@
     start_all(gu_copies(0))
     start_all(down_copies(0))
 
+    gain_s[0] = ga_ref[...].astype(F32)
+    gain_s[1] = gm_ref[...].astype(F32)
+
     barrier = pltpu.get_barrier_semaphore()
-    for stride in (1, 4, 16):
-        for delta in (1, 2, 3):
-            pl.semaphore_signal(barrier, inc=1, device_id={'sp': neighbour(stride, delta), 'tp': tp}, device_id_type=MESH)
+    for way in zip(AXIS_STRIDE, axis_at):
+        for delta in (NEXT, FAR, PREV):
+            pl.semaphore_signal(barrier, inc=1, device_id={'sp': ring_to(way, delta), 'tp': tp}, device_id_type=MESH)
     pl.semaphore_signal(barrier, inc=1, device_id={'sp': sp, 'tp': 1 - tp}, device_id_type=MESH)
     pl.semaphore_wait(barrier, 10)
 
@@ -115,55 +129,65 @@
     remote(aux_ref, aux_buf.at[:, theirs], ini_ss.at[1], ini_rs.at[1], sp, 1 - tp).wait_recv()
 
     seg_col = aux_buf[2]
-    lane_f = lax.broadcasted_iota(jnp.int32, (rows, 128), 1).astype(F32)
+    lane_f = lax.broadcasted_iota(jnp.int32, (rows, LANES), 1).astype(F32)
     below = jnp.sum(jnp.where(seg_col < lane_f, 1.0, 0.0), axis=0, keepdims=True)
     upto = jnp.sum(jnp.where(seg_col < lane_f + 1.0, 1.0, 0.0), axis=0, keepdims=True)
-    mx, my, mz = coord(1), coord(4), coord(16)
+    mx, my, mz = axis_at
     cnt_buf[mz, my, mx] = jnp.concatenate([jnp.broadcast_to(below, (8, 128)), jnp.broadcast_to(upto, (8, 128))], axis=0)
-    for phase, stride in enumerate((1, 4, 16)):
-        def block(cz, cy, cx):
-            return (cnt_buf.at[cz, cy, cx], cnt_buf.at[cz, cy], cnt_buf.at[cz])[phase]
-        for delta in (1, 2, 3):
-            b = block(mz, my, mx)
+
+    def count_block(phase, cz, cy, cx):
+        return (cnt_buf.at[cz, cy, cx], cnt_buf.at[cz, cy], cnt_buf.at[cz])[phase]
+
+    def count_send(phase):
+        for delta in (NEXT, FAR, PREV):
+            b = count_block(phase, mz, my, mx)
             i = phase * 3 + delta - 1
-            remote(b, b, cnt_ss.at[i], cnt_rs.at[i], neighbour(stride, delta), tp).start()
-        for delta in (1, 2, 3):
+            remote(b, b, cnt_ss.at[i], cnt_rs.at[i], ring_to((AXIS_STRIDE[phase], axis_at[phase]), delta), tp).start()
+
+    def count_phase(phase):
+        for delta in (NEXT, FAR, PREV):
             i = phase * 3 + delta - 1
             frm = [mz, my, mx]
             frm[2 - phase] = (frm[2 - phase] - delta) % 4
-            b = block(*frm)
-            c = remote(b, b, cnt_ss.at[i], cnt_rs.at[i], neighbour(stride, delta), tp)
+            b = count_block(phase, *frm)
+            c = remote(b, b, cnt_ss.at[i], cnt_rs.at[i], ring_to((AXIS_STRIDE[phase], axis_at[phase]), delta), tp)
             c.wait_send()
             c.wait_recv()
-    total = jnp.sum(cnt_buf[...].reshape(64, 16, 128), axis=0)
-    seg_lo = total[0:1, :]
-    seg_hi = total[8:9, :]
-
-    for p in range(3):
-        s1, s2, s3 = PART_STRIDES[p]
-        pr = PART_ROWS[p]
-        row_i = lax.broadcasted_iota(jnp.int32, (pr, 128), 0)
-        lane_i = lax.broadcasted_iota(jnp.int32, (pr, 128), 1)
-
-        def fill(b, carry, p=p, s1=s1, s2=s2, s3=s3, pr=pr, row_i=row_i, lane_i=lane_i):
-            c3 = b // 16
-            c2 = (b // 4) % 4
-            c1 = b % 4
-            blk = c3 * s3 + c2 * s2 + c1 * s1
-            idx = (row_i + (blk * rows + PART_OFF[p])).astype(F32)
-            one_hot = jnp.where(idx >= seg_lo, 1.0, 0.0) * jnp.where(idx < seg_hi, 1.0, 0.0)
-            late = jnp.where(row_i * 0 + blk >= sp, 1.0, 0.0)
-            val = jnp.where(lane_i < 4, one_hot, jnp.where(lane_i == 4, late, 0.0))
-            exts[p][c3, c2, c1] = val.astype(BF16)
-            return carry
-        lax.fori_loop(0, 64, fill, 0)
+        if phase < 2:
+            count_send(phase + 1)
+
+    count_send(0)
+
+    def fill_exts():
+        total = jnp.sum(cnt_buf[...].reshape(64, 16, 128), axis=0)
+        seg_lo = total[0:1, :]
+        seg_hi = total[8:9, :]
+        for p in range(3):
+            (s1, _), (s2, _), (s3, _) = ways[p]
+            pr = PART_ROWS[p]
+            row_i = lax.broadcasted_iota(jnp.int32, (pr, LANES), 0)
+            lane_i = lax.broadcasted_iota(jnp.int32, (pr, LANES), 1)
+            row_f = row_i.astype(F32)
+
+            def fill(b, carry, p=p, s1=s1, s2=s2, s3=s3, pr=pr, row_i=row_i, lane_i=lane_i, row_f=row_f):
+                for c1 in range(4):
+                    c3 = b // 4
+                    c2 = b % 4
+                    blk = c3 * s3 + c2 * s2 + c1 * s1
+                    idx = (row_i + (blk * rows + PART_OFF[p])).astype(F32)
+                    one_hot = jnp.where(idx >= seg_lo, 1.0, 0.0) * jnp.where(idx < seg_hi, 1.0, 0.0)
+                    late = jnp.where(row_i * 0 + blk >= sp, 1.0, 0.0)
+                    val = jnp.where(lane_i < 4, one_hot, jnp.where(lane_i == 4, late, 0.0))
+                    exts[p][c3, c2, c1] = val.astype(BF16)
+                return carry
+            lax.fori_loop(0, 16, fill, 0)
 
     seg_row = jnp.transpose(seg_col)
-    row_i = lax.broadcasted_iota(jnp.int32, (rows, 128), 0)
-    col_i = lax.broadcasted_iota(jnp.int32, (rows, 128), 1)
+    row_i = lax.broadcasted_iota(jnp.int32, (rows, LANES), 0)
+    col_i = lax.broadcasted_iota(jnp.int32, (rows, LANES), 1)
     q_side = jnp.where(row_i < 4, jnp.where(seg_row == row_i.astype(F32), 0.0, -BIG), jnp.where(row_i == 4, -BIG, 0.0)).astype(BF16)
     for h in range(n_heads):
-        q_t[128:256, h * 128:(h + 1) * 128] = q_side
+        q_t[128:256, h * LANES:(h + 1) * LANES] = q_side
     mask_add[...] = jnp.where(row_i <= col_i, jnp.where(seg_col == seg_row, 0.0, -BIG), -BIG)
 
     def soft_step(keys, vals, cols, add, first):
@@ -191,21 +215,46 @@
         m_s[:, cols] = jnp.broadcast_to(m_new, (8, n_c))
         l_s[:, cols] = jnp.broadcast_to(l_new, (8, n_c))
 
+    base2 = 3
+    base3 = base2 + RING
+    first_two = pl.ds(0, 2)
+    last_two = pl.ds(2, 2)
     col_tiles = [slice(c, c + 256) for c in range(0, n_q, 256)]
 
-    def plane_step(p, par, c3):
-        n_k = 16 * PART_ROWS[p]
-        kv = kvs[p][par, c3].reshape(n_k, 256)
-        keys = jnp.concatenate([kv[:, 0:128], exts[p][c3].reshape(n_k, 128)], axis=1)
-        for cols in col_tiles:
-            soft_step(keys, kv[:, 128:256], cols, None, False)
+    def row_step(par, coords, o3, o2):
+        kv_rows, ext_rows = [], []
+        for p in range(3):
+            m1, m2, m3 = coords[p]
+            c3 = (m3 + o3) % RING
+            c2 = (m2 + o2) % RING
+            n_k = 4 * PART_ROWS[p]
+            kv_rows.append(kvs[p][par, c3, c2].reshape(n_k, 256))
+            ext_rows.append(exts[p][c3, c2].reshape(n_k, 128))
+        kv = jnp.concatenate(kv_rows, axis=0)
+        keys = jnp.concatenate([kv[:, 0:128], jnp.concatenate(ext_rows, axis=0)], axis=1)
+        vals = kv[:, 128:256]
+        m_old = [m_s[0:1, cols] for cols in col_tiles]
+        l_old = [l_s[0:1, cols] for cols in col_tiles]
+        half = keys.shape[0] // 2
+        parts = (slice(0, half), slice(half, 2 * half))
+        ss = [[jnp.dot(keys[r], q_t[:, cols], preferred_element_type=F32) for r in parts] for cols in col_tiles]
+        m_new = [jnp.maximum(a, jnp.max(jnp.maximum(b[0], b[1]), axis=0, keepdims=True)) for a, b in zip(m_old, ss)]
+        es = [[jnp.exp2((b - a) * EXP_SCALE) for b in bs] for a, bs in zip(m_new, ss)]
+        al = [jnp.exp2((a - b) * EXP_SCALE) for a, b in zip(m_old, m_new)]
+        vt = jnp.transpose(vals)
+        pvs = [jnp.dot(vt[:, 0:half], e[0].astype(BF16), preferred_element_type=F32) + jnp.dot(vt[:, half:], e[1].astype(BF16), preferred_element_type=F32) for e in es]
+        for i, cols in enumerate(col_tiles):
+            l_new = l_old[i] * al[i] + jnp.sum(es[i][0] + es[i][1], axis=0, keepdims=True)
+            acc_s[:, cols] = acc_s[:, cols] * al[i] + pvs[i]
+            m_s[:, cols] = jnp.broadcast_to(m_new[i], (8, 256))
+            l_s[:, cols] = jnp.broadcast_to(l_new, (8, 256))
 
     def layer_step(layer, carry):
         par = layer % 2
         has_next = layer + 1 < n_layers
 
-        def send(p, i, ref, stride, delta):
-            remote(ref, ref, g_ss.at[p, i], g_rs.at[par, p, i], neighbour(stride, delta), tp).start()
+        def send(p, i, ref, dim, delta):
+            remote(ref, ref, g_ss.at[p, i], g_rs.at[par, p, i], ring_to(ways[p][dim], delta), tp).start()
 
         def got(p, i, ref):
             remote(ref, ref, g_ss.at[p, i], g_rs.at[par, p, i], sp, 1 - tp).wait_recv()
@@ -213,9 +262,12 @@
         def sent(p, i, ref):
             remote(ref, ref, g_ss.at[p, i], g_rs.at[par, p, i], sp, 1 - tp).wait_send()
 
-        coords = [tuple(coord(s) for s in PART_STRIDES[p]) for p in range(3)]
-
-        n_s[...] = rms_rows(x_buf[...], ga_ref[layer])
+        def first_layer(step, *a):
+            @pl.when(layer == 0)
+            def _():
+                step(*a)
+
+        n_s[...] = rms_rows(x_buf[...], gain_s[0, pl.ds(layer, 1), :])
         wait_all(qkv_copies(layer))
         cos_t = aux_buf[0]
         sin_t = aux_buf[1]
@@ -237,86 +289,97 @@
         start_all(cache)
         for p in range(3):
             m1, m2, m3 = coords[p]
-            own = kvs[p].at[par, m3, m2, m1]
-            for i, delta in enumerate((1, 3, 2)):
-                send(p, i, own, PART_STRIDES[p][0], delta)
+            for delta in (FAR, NEXT, PREV):
+                send(p, delta - 1, kvs[p].at[par, m3, m2, m1], 0, delta)
         q_lin = jnp.dot(n_s[...], wqkv[:, 0:n_q], preferred_element_type=F32)
         for h in range(n_heads):
-            q_h = rope(q_lin[:, h * 128:(h + 1) * 128])
-            q_t[0:128, h * 128:(h + 1) * 128] = jnp.transpose(q_h)
+            q_h = rope(q_lin[:, h * LANES:(h + 1) * LANES])
+            q_t[0:128, h * LANES:(h + 1) * LANES] = jnp.transpose(q_h)
 
         @pl.when(has_next)
         def _():
             start_all(qkv_copies(layer + 1))
 
+        first_layer(count_phase, 0)
+
         mask2 = jnp.concatenate([mask_add[...], mask_add[...]], axis=1)
         for cols in col_tiles:
             soft_step(kst[...], vst[...], cols, mask2, True)
 
+        first_layer(count_phase, 1)
+        def ring_sends(p, base, dim, ref):
+            send(p, base, ref, dim, NEXT)
+            send(p, base + 1, ref, dim, PREV)
+
+        def row_sems(off):
+            return base3 + RING * off
+
         for p in range(3):
             m1, m2, m3 = coords[p]
-            s1, s2, s3 = PART_STRIDES[p]
-            for i, delta in enumerate((1, 3, 2)):
-                got(p, i, kvs[p].at[par, m3, m2, (m1 - delta) % 4])
+            for delta in (NEXT, PREV, FAR):
+                got(p, delta - 1, kvs[p].at[par, m3, m2, (m1 - delta) % RING])
             row = kvs[p].at[par, m3, m2]
-            send(p, 3, row, s2, 1)
-            send(p, 4, row, s2, 3)
-            send(p, 7, row, s3, 1)
-            send(p, 8, row, s3, 3)
-
-        def pass_on3(p, r, c2):
+            ring_sends(p, base2, 1, row)
+            ring_sends(p, row_sems(OWN), 2, row)
+        first_layer(count_phase, 2)
+        first_layer(fill_exts)
+        row_step(par, coords, OWN, OWN)
+
+        def ring_pass(p, base, dim, prev, nxt):
+            got(p, base, prev)
+            send(p, base + 2, prev.at[first_two], dim, NEXT)
+            got(p, base + 1, nxt)
+            send(p, base + 3, nxt.at[last_two], dim, PREV)
+
+        def ring_far(p, base, far):
+            got(p, base + 2, far.at[first_two])
+            got(p, base + 3, far.at[last_two])
+
+        def row_at(p, o3, o2):
             m1, m2, m3 = coords[p]
-            s3 = PART_STRIDES[p][2]
-            lo = (m3 - 1) % 4
-            hi = (m3 + 1) % 4
-            got(p, 7 + 4 * r, kvs[p].at[par, lo, c2])
-            send(p, 9 + 4 * r, kvs[p].at[par, lo, c2, 0:2], s3, 1)
-            got(p, 8 + 4 * r, kvs[p].at[par, hi, c2])
-            send(p, 10 + 4 * r, kvs[p].at[par, hi, c2, 2:4], s3, 3)
-
-        for p in range(3):
-            m1, m2, m3 = coords[p]
-            s1, s2, s3 = PART_STRIDES[p]
-            lo = (m2 - 1) % 4
-            hi = (m2 + 1) % 4
-            got(p, 3, kvs[p].at[par, m3, lo])
-            send(p, 5, kvs[p].at[par, m3, lo, 0:2], s2, 1)
-            send(p, 11, kvs[p].at[par, m3, lo], s3, 1)
-            send(p, 12, kvs[p].at[par, m3, lo], s3, 3)
-            got(p, 4, kvs[p].at[par, m3, hi])
-            send(p, 6, kvs[p].at[par, m3, hi, 2:4], s2, 3)
-            send(p, 15, kvs[p].at[par, m3, hi], s3, 1)
-            send(p, 16, kvs[p].at[par, m3, hi], s3, 3)
-        for p in range(3):
-            pass_on3(p, 0, coords[p][1])
-        for p in range(3):
-            m1, m2, m3 = coords[p]
-            s1, s2, s3 = PART_STRIDES[p]
-            far = (m2 + 2) % 4
-            got(p, 5, kvs[p].at[par, m3, far, 0:2])
-            got(p, 6, kvs[p].at[par, m3, far, 2:4])
-            send(p, 19, kvs[p].at[par, m3, far], s3, 1)
-            send(p, 20, kvs[p].at[par, m3, far], s3, 3)
-        for p in range(3):
-            plane_step(p, par, coords[p][2])
-        for r, off in ((1, 3), (2, 1), (3, 2)):
+            return kvs[p].at[par, (m3 + o3) % RING, (m2 + o2) % RING]
+
+        def pass_on3(off):
             for p in range(3):
-                pass_on3(p, r, (coords[p][1] + off) % 4)
-        for p in range(3):
-            plane_step(p, par, (coords[p][2] + 3) % 4)
-        for p in range(3):
-            plane_step(p, par, (coords[p][2] + 1) % 4)
-        for p in range(3):
-            m1, m2, m3 = coords[p]
-            far = (m3 + 2) % 4
-            for r, off in ((0, 0), (1, 3), (2, 1), (3, 2)):
-                c2 = (m2 + off) % 4
-                got(p, 9 + 4 * r, kvs[p].at[par, far, c2, 0:2])
-                got(p, 10 + 4 * r, kvs[p].at[par, far, c2, 2:4])
-            plane_step(p, par, far)
+                ring_pass(p, row_sems(off), 2, row_at(p, PREV, off), row_at(p, NEXT, off))
+
+        def far3(off):
+            for p in range(3):
+                ring_far(p, row_sems(off), row_at(p, FAR, off))
+
+        for p in range(3):
+            ring_pass(p, base2, 1, row_at(p, OWN, PREV), row_at(p, OWN, NEXT))
+            for off in (PREV, NEXT):
+                ring_sends(p, row_sems(off), 2, row_at(p, OWN, off))
+        row_step(par, coords, OWN, PREV)
+        pass_on3(OWN)
+        row_step(par, coords, OWN, NEXT)
+        for p in range(3):
+            ring_far(p, base2, row_at(p, OWN, FAR))
+            ring_sends(p, row_sems(FAR), 2, row_at(p, OWN, FAR))
+        row_step(par, coords, PREV, OWN)
+        row_step(par, coords, NEXT, OWN)
+        pass_on3(PREV)
+        row_step(par, coords, OWN, FAR)
+        row_step(par, coords, PREV, PREV)
+        pass_on3(NEXT)
+        row_step(par, coords, NEXT, PREV)
+        far3(OWN)
+        row_step(par, coords, FAR, OWN)
+        row_step(par, coords, PREV, NEXT)
+        pass_on3(FAR)
+        row_step(par, coords, NEXT, NEXT)
+        row_step(par, coords, PREV, FAR)
+        row_step(par, coords, NEXT, FAR)
+        far3(PREV)
+        row_step(par, coords, FAR, PREV)
+        far3(NEXT)
+        row_step(par, coords, FAR, NEXT)
+        far3(FAR)
+        row_step(par, coords, FAR, FAR)
 
         for h in range(n_heads):
-            cols = slice(h * 128, (h + 1) * 128)
+            cols = slice(h * LANES, (h + 1) * LANES)
             o_t = acc_s[:, cols] * (1.0 / l_s[0:1, cols])
             o_s[:, cols] = jnp.transpose(o_t.astype(BF16))
         wait_all(wo_copies(layer))
@@ -331,17 +394,13 @@
 
         for p in range(3):
             m1, m2, m3 = coords[p]
-            for i in range(3):
-                sent(p, i, kvs[p].at[par, m3, m2, m1])
-            for i in (3, 4):
-                sent(p, i, kvs[p].at[par, m3, m2])
-            for i in (5, 6):
-                sent(p, i, kvs[p].at[par, m3, m2, 0:2])
-            for r in range(4):
-                for i in (7, 8):
-                    sent(p, i + 4 * r, kvs[p].at[par, m3, m2])
-                for i in (9, 10):
-                    sent(p, i + 4 * r, kvs[p].at[par, m3, m2, 0:2])
+            row = kvs[p].at[par, m3, m2]
+            for i in range(base2):
+                sent(p, i, row.at[m1])
+            for base in (base2, *map(row_sems, range(RING))):
+                for i in range(2):
+                    sent(p, base + i, row)
+                    sent(p, base + 2 + i, row.at[first_two])
 
         @pl.when(has_next)
         def _():
@@ -353,7 +412,7 @@
             res = (snd_a[t].astype(F32) + rcv_a[t].astype(F32)).astype(BF16)
             x_buf[:, cols] = (x_buf[:, cols].astype(F32) + res.astype(F32)).astype(BF16)
 
-        n_s[...] = rms_rows(x_buf[...], gm_ref[layer])
+        n_s[...] = rms_rows(x_buf[...], gain_s[1, pl.ds(layer, 1), :])
         wait_all(gu_copies(layer))
 
         def gate_up(cols):
@@ -436,14 +495,10 @@
                 pltpu.VMEM((d_model, ffn), BF16),
                 pltpu.VMEM((d_model, ffn), BF16),
                 pltpu.VMEM((ffn, d_model), BF16),
-                pltpu.VMEM((2, 4, 4, 4, PART_ROWS[0], 256), BF16),
-                pltpu.VMEM((2, 4, 4, 4, PART_ROWS[1], 256), BF16),
-                pltpu.VMEM((2, 4, 4, 4, PART_ROWS[2], 256), BF16),
-                pltpu.VMEM((4, 4, 4, PART_ROWS[0], 128), BF16),
-                pltpu.VMEM((4, 4, 4, PART_ROWS[1], 128), BF16),
-                pltpu.VMEM((4, 4, 4, PART_ROWS[2], 128), BF16),
+                *[pltpu.VMEM((2, RING, RING, RING, r, 2 * LANES), BF16) for r in PART_ROWS],
+                *[pltpu.VMEM((RING, RING, RING, r, LANES), BF16) for r in PART_ROWS],
                 pltpu.VMEM((256, n_q), BF16),
-                pltpu.VMEM((rows, 128), F32),
+                pltpu.VMEM((rows, LANES), F32),
                 pltpu.VMEM((8, n_q), F32),
                 pltpu.VMEM((8, n_q), F32),
                 pltpu.VMEM((HEAD_DIM, n_q), F32),
@@ -456,11 +511,12 @@
                 pltpu.VMEM((n_t, rows, tw), BF16),
                 pltpu.VMEM((n_t, rows, tw), BF16),
                 pltpu.VMEM((n_t, rows, tw), BF16),
+                pltpu.VMEM((2, n_layers, d_model), F32),
                 dma((2,)), dma((2,)), dma((9,)), dma((9,)), dma((16,)),
                 dma((3, N_SEM)), dma((2, 3, N_SEM)), dma((2, n_t)), dma((2, n_t)), dma((2,)),
             ],
             compiler_params=pltpu.CompilerParams(collective_id=0, has_side_effects=True, vmem_limit_bytes=67043328),
-        )(hidden_in, aux, attn_gain.astype(F32)[:, None, :], mlp_gain.astype(F32)[:, None, :], w_q, w_k, w_v, w_o, w_gate, w_up, w_down)
+        )(hidden_in, aux, attn_gain, mlp_gain, w_q, w_k, w_v, w_o, w_gate, w_up, w_down)
         return hid, k_c.reshape(n_layers, rows, 1, HEAD_DIM), v_c.reshape(n_layers, rows, 1, HEAD_DIM)
 
     return jax.shard_map(device_fn, mesh=mesh,

time: 413 us -> 337 us (0.82)
  Pallas kernels: 402 us -> 329 us
    pallas_call x1, Pallas kernels: 402 us -> 329 us  [device_fn(): pl.pallas_call(body, out_shape=(jax.ShapeDtypeStruct((half_rows, d_model)...]
where the time goes in v2:
time: 337 us
  Pallas kernels  329 us (98%)
  local copies, waits for them, and re-layouts  5.03 us (1%)
    pallas_call x1, Pallas kernels, device_fn(): pl.pallas_call(body, out_shape=(jax.ShapeDtypeStruct((half_rows, d_model)...  329 us

profile of v2, /device:TPU:1, one launch (start us, length us, event | category | flops | bytes accessed | tf_op | source)
XLA Modules:
  0.0 337.2 jit_solution(7999637643658494516)
XLA Ops:
  0.6 0.7 convert_element_type.7
  1.3 0.7 convert_element_type.6
  2.0 0.1 stack_broadcast_in_dim.2
  2.0 0.2 multiply_cosine_fusion
  2.2 0.1 maximum_bitcast_fusion
  2.3 0.6 pad_maximum_fusion.refs_1_
  3.0 329.3 %shard_map.139 = (bf16[64,1536]{1,0:T(8,128)(2,1)}, bf16[8,128,128]{2,1,0:T(8,128)(2,1)}, bf16[8,128,128]{2,1,0:T(8,128)(2,1)}) custom-call(bf16[64,1536]{1,0:T(8,128)(2,1)} %refs_0_.1, f32[3,64,128]{2,1,0:T(8,128)} %pad_maximum_fusion.refs_1_, bf16[8,1536]{1,0:T(8,128)(2,1)} %refs_2_.1, bf16[8,1536]{1,0:T(8,128)(2,1)} %refs_3_.1, ...), custom_call_target="tpu_custom_call" | custom-call | tf_op jit(solution)/shard_map/pallas_call | solution.py:482
  332.3 1.6 copy.20
  333.9 1.7 copy.21
  335.6 1.7 copy.22
  (1 shorter events, 0.0 us)

commit v3 on v2

--- a/solution.py
+++ b/solution.py
@@ -20,7 +20,7 @@
 PART_OFF = (0, 48, 96)
 X, Y, Z = range(3)
 AXIS_STRIDE = (1, 4, 16)
-PART_AXES = (((X, Y, Z), (Y, Z, X), (X, Z, Y)), ((Z, Y, X), (X, Z, Y), (X, Y, Z)))
+PART_AXES = (((X, Y, Z), (Y, Z, X), (Z, X, Y)), ((Y, Z, X), (Z, X, Y), (X, Y, Z)))
 N_SEM = 23
 OWN, NEXT, FAR, PREV = range(4)
 RING = 4
@@ -221,15 +221,16 @@
     last_two = pl.ds(2, 2)
     col_tiles = [slice(c, c + 256) for c in range(0, n_q, 256)]
 
-    def row_step(par, coords, o3, o2):
+    def row_step(par, coords, *offs):
         kv_rows, ext_rows = [], []
-        for p in range(3):
-            m1, m2, m3 = coords[p]
-            c3 = (m3 + o3) % RING
-            c2 = (m2 + o2) % RING
-            n_k = 4 * PART_ROWS[p]
-            kv_rows.append(kvs[p][par, c3, c2].reshape(n_k, 256))
-            ext_rows.append(exts[p][c3, c2].reshape(n_k, 128))
+        for o3, o2 in offs:
+            for p in range(3):
+                m1, m2, m3 = coords[p]
+                c3 = (m3 + o3) % RING
+                c2 = (m2 + o2) % RING
+                n_k = RING * PART_ROWS[p]
+                kv_rows.append(kvs[p][par, c3, c2].reshape(n_k, 256))
+                ext_rows.append(exts[p][c3, c2].reshape(n_k, LANES))
         kv = jnp.concatenate(kv_rows, axis=0)
         keys = jnp.concatenate([kv[:, 0:128], jnp.concatenate(ext_rows, axis=0)], axis=1)
         vals = kv[:, 128:256]
@@ -241,13 +242,12 @@
         m_new = [jnp.maximum(a, jnp.max(jnp.maximum(b[0], b[1]), axis=0, keepdims=True)) for a, b in zip(m_old, ss)]
         es = [[jnp.exp2((b - a) * EXP_SCALE) for b in bs] for a, bs in zip(m_new, ss)]
         al = [jnp.exp2((a - b) * EXP_SCALE) for a, b in zip(m_old, m_new)]
-        vt = jnp.transpose(vals)
+        vt = jnp.concatenate([jnp.transpose(vals), jnp.ones((16, 2 * half), BF16)], axis=0)
         pvs = [jnp.dot(vt[:, 0:half], e[0].astype(BF16), preferred_element_type=F32) + jnp.dot(vt[:, half:], e[1].astype(BF16), preferred_element_type=F32) for e in es]
         for i, cols in enumerate(col_tiles):
-            l_new = l_old[i] * al[i] + jnp.sum(es[i][0] + es[i][1], axis=0, keepdims=True)
-            acc_s[:, cols] = acc_s[:, cols] * al[i] + pvs[i]
+            acc_s[:, cols] = acc_s[:, cols] * al[i] + pvs[i][0:LANES]
+            l_s[:, cols] = l_s[:, cols] * al[i] + pvs[i][LANES:LANES + 8]
             m_s[:, cols] = jnp.broadcast_to(m_new[i], (8, 256))
-            l_s[:, cols] = jnp.broadcast_to(l_new, (8, 256))
 
     def layer_step(layer, carry):
         par = layer % 2
@@ -323,7 +323,7 @@
             ring_sends(p, row_sems(OWN), 2, row)
         first_layer(count_phase, 2)
         first_layer(fill_exts)
-        row_step(par, coords, OWN, OWN)
+        row_step(par, coords, (OWN, OWN))
 
         def ring_pass(p, base, dim, prev, nxt):
             got(p, base, prev)
@@ -351,32 +351,29 @@
             ring_pass(p, base2, 1, row_at(p, OWN, PREV), row_at(p, OWN, NEXT))
             for off in (PREV, NEXT):
                 ring_sends(p, row_sems(off), 2, row_at(p, OWN, off))
-        row_step(par, coords, OWN, PREV)
+        row_step(par, coords, (OWN, PREV))
         pass_on3(OWN)
-        row_step(par, coords, OWN, NEXT)
+        row_step(par, coords, (OWN, NEXT))
         for p in range(3):
             ring_far(p, base2, row_at(p, OWN, FAR))
             ring_sends(p, row_sems(FAR), 2, row_at(p, OWN, FAR))
-        row_step(par, coords, PREV, OWN)
-        row_step(par, coords, NEXT, OWN)
+        row_step(par, coords, (PREV, OWN), (NEXT, OWN))
         pass_on3(PREV)
-        row_step(par, coords, OWN, FAR)
-        row_step(par, coords, PREV, PREV)
+        row_step(par, coords, (OWN, FAR))
+        row_step(par, coords, (PREV, PREV))
         pass_on3(NEXT)
-        row_step(par, coords, NEXT, PREV)
+        row_step(par, coords, (NEXT, PREV))
         far3(OWN)
-        row_step(par, coords, FAR, OWN)
-        row_step(par, coords, PREV, NEXT)
+        row_step(par, coords, (FAR, OWN))
+        row_step(par, coords, (PREV, NEXT))
         pass_on3(FAR)
-        row_step(par, coords, NEXT, NEXT)
-        row_step(par, coords, PREV, FAR)
-        row_step(par, coords, NEXT, FAR)
+        row_step(par, coords, (NEXT, NEXT))
+        row_step(par, coords, (PREV, FAR), (NEXT, FAR))
         far3(PREV)
-        row_step(par, coords, FAR, PREV)
         far3(NEXT)
-        row_step(par, coords, FAR, NEXT)
+        row_step(par, coords, (FAR, PREV), (FAR, NEXT))
         far3(FAR)
-        row_step(par, coords, FAR, FAR)
+        row_step(par, coords, (FAR, FAR))
 
         for h in range(n_heads):
             cols = slice(h * LANES, (h + 1) * LANES)
@@ -454,6 +451,12 @@
 
     lax.fori_loop(0, n_layers, layer_step, 0)
     hid_out[...] = x_buf[mine, :]
+
+
+def hand_over(a_ref, b_ref, c_ref, a_out, b_out, c_out):
+    a_out[...] = a_ref[...]
+    b_out[...] = b_ref[...]
+    c_out[...] = c_ref[...]
 
 
 def solution(mesh):
@@ -517,6 +520,9 @@
             ],
             compiler_params=pltpu.CompilerParams(collective_id=0, has_side_effects=True, vmem_limit_bytes=67043328),
         )(hidden_in, aux, attn_gain, mlp_gain, w_q, w_k, w_v, w_o, w_gate, w_up, w_down)
+        hid, k_c, v_c = pl.pallas_call(
+            hand_over, out_shape=tuple(jax.ShapeDtypeStruct(r.shape, r.dtype) for r in (hid, k_c, v_c)),
+            in_specs=[vm] * 3, out_specs=(vm, vm, vm))(hid, k_c, v_c)
         return hid, k_c.reshape(n_layers, rows, 1, HEAD_DIM), v_c.reshape(n_layers, rows, 1, HEAD_DIM)
 
     return jax.shard_map(device_fn, mesh=mesh,

time: 337 us -> 322 us (0.955)
  Pallas kernels: 329 us -> 319 us
  local copies, waits for them, and re-layouts: 5.03 us -> 0.07 us
    pallas_call x1, Pallas kernels: 329 us -> 317 us  [device_fn(): pl.pallas_call(body, out_shape=(jax.ShapeDtypeStruct((half_rows, d_model)...]
    unnamed x3 -> x0, local copies, waits for them, and re-layouts: 4.96 us -> none
where the time goes in v3:
time: 322 us
  Pallas kernels  319 us (99%)
    pallas_call x1, Pallas kernels, device_fn(): pl.pallas_call(body, out_shape=(jax.ShapeDtypeStruct((half_rows, d_model)...  317 us

profile of v3, /device:TPU:1, one launch (start us, length us, event | category | flops | bytes accessed | tf_op | source)
XLA Modules:
  0.0 322.0 jit_solution(6799259956813784661)
XLA Ops:
  0.6 0.7 convert_element_type.7
  1.3 0.7 convert_element_type.6
  2.0 0.1 stack_broadcast_in_dim.2
  2.0 0.2 multiply_cosine_fusion
  2.2 0.1 maximum_bitcast_fusion
  2.3 0.6 pad_maximum_fusion.refs_1_
  3.0 317.0 %shard_map.139 = (bf16[64,1536]{1,0:T(8,128)(2,1)}, bf16[8,128,128]{2,1,0:T(8,128)(2,1)}, bf16[8,128,128]{2,1,0:T(8,128)(2,1)}) custom-call(bf16[64,1536]{1,0:T(8,128)(2,1)} %refs_0_.1, f32[3,64,128]{2,1,0:T(8,128)} %pad_maximum_fusion.refs_1_, bf16[8,1536]{1,0:T(8,128)(2,1)} %refs_2_.1, bf16[8,1536]{1,0:T(8,128)(2,1)} %refs_3_.1, ...), custom_call_target="tpu_custom_call" | custom-call | tf_op jit(solution)/shard_map/pallas_call | solution.py:485
  320.0 2.0 shard_map.140
  (1 shorter events, 0.0 us)
